TPU v7x, 32 devices: a whole 2x2x4 slice. The times are simulated.
32 devices in a mesh: gx: 4 (over z), gy: 4 (over x, core), gz: 2 (over y).
Axes of the slice: x: 2, y: 2, z: 4, core: 2. Of those that a mesh axis runs over, the one named last changes fastest.
Arguments:
- populations: float32 [19, 16, 32, 512], P(None, 'gz', 'gx', 'gy'), may hold values from 0 to 1, as said below
- omega: float32 [16, 32, 512], P('gz', 'gx', 'gy'), may hold values from 0.8 to 1.7
- obstacle: int32 [16, 32, 512], P('gz', 'gx', 'gy'), may hold values 0 or 1
Outputs:
- lifted: float32 [19, 16, 32, 512], P(None, 'gz', 'gx', 'gy')
- diagnostics: float32 [5], replicated
Inputs may be any that keep to these rules, and one draw needn't show every extreme that they name: `populations`: every population lies between 0.3 and 1.7 times its lattice weight.
All inputs are finite; a program needn't handle non-finite values. No bound on the sum of `obstacle` on one device may be relied on, other than what follows from the above.
Results may differ from a plain program's by a relative error of at most 0.0001.
Values sent between devices are 32-bit elements; how exact they have to be, the bound alone decides.
A program may use at most 128 MiB of HBM per device.

v0:
```python
import jax
import jax.numpy as jnp
from jax import lax
from jax.sharding import PartitionSpec as P

STEPS = 4
JUMP = 2


lattice = [
    (0, 0, 0),
    (1, 0, 0),
    (-1, 0, 0),
    (0, 1, 0),
    (0, -1, 0),
    (0, 0, 1),
    (0, 0, -1),
    (1, 1, 0),
    (-1, -1, 0),
    (1, -1, 0),
    (-1, 1, 0),
    (1, 0, 1),
    (-1, 0, -1),
    (1, 0, -1),
    (-1, 0, 1),
    (0, 1, 1),
    (0, -1, -1),
    (0, 1, -1),
    (0, -1, 1),
]
weights = [1.0 / 3.0] + [1.0 / 18.0] * 6 + [1.0 / 36.0] * 12
opposite = [0, 2, 1, 4, 3, 6, 5, 8, 7, 10, 9, 12, 11, 14, 13, 16, 15, 18, 17]
limiter = 25.0


def extended(x, sides, width):
    for axis, dim in sides:
        size, length = (lax.axis_size(axis), x.shape[dim])
        up = [(i, (i + 1) % size) for i in range(size)]
        down = [(j, i) for i, j in up]
        last = lax.slice_in_dim(x, length - width, length, axis=dim)
        first = lax.slice_in_dim(x, 0, width, axis=dim)
        before = lax.ppermute(last, axis, up)
        after = lax.ppermute(first, axis, down)
        x = jnp.concatenate([before, x, after], axis=dim)
    return x


def moments(f):
    rho = jnp.sum(f, axis=0)
    comps = []
    for axis_pick in range(3):
        total = jnp.zeros_like(rho)
        for index in range(19):
            comp = lattice[index][axis_pick]
            if comp != 0:
                total = total + comp * f[index]
        comps.append(total)
    return (rho, comps[0], comps[1], comps[2])


def equilibrium(rho, momx, momy, momz):
    safe = jnp.maximum(rho, 0.5)
    velx, vely, velz = (momx / safe, momy / safe, momz / safe)
    square = velx * velx + vely * vely + velz * velz
    rows = []
    for index in range(19):
        cx, cy, cz = lattice[index]
        proj = cx * velx + cy * vely + cz * velz
        rows.append(weights[index] * rho * (1.0 + 3.0 * proj + 4.5 * proj * proj - 1.5 * square))
    return jnp.stack(rows, 0)


def collide(f, omega, solid):
    rho, momx, momy, momz = moments(f)
    feq = equilibrium(rho, momx, momy, momz)
    post = f + omega[None] * (feq - f)
    flipped = jnp.stack([f[opposite[index]] for index in range(19)], 0)
    return jnp.where(solid[None], flipped, post)


def stream(padded):
    size_z = padded.shape[1] - 2
    size_x = padded.shape[2] - 2
    size_y = padded.shape[3] - 2
    rows = []
    for index in range(19):
        cx, cy, cz = lattice[index]
        rows.append(
            padded[
                index, 1 - cz : 1 - cz + size_z, 1 - cx : 1 - cx + size_x, 1 - cy : 1 - cy + size_y
            ]
        )
    return jnp.stack(rows, 0)


def per_device(populations, omega, obstacle):
    solid = obstacle == 1
    f = populations
    before = f
    for step in range(STEPS):
        post = collide(f, omega, solid)
        padded = extended(post, (("gx", 2), ("gy", 3), ("gz", 1)), 1)
        f = stream(padded)
        if step == STEPS - 2:
            before = f
    rho_a, jxa, jya, jza = moments(before)
    rho_b, jxb, jyb, jzb = moments(f)
    cells = float(
        f.shape[1]
        * f.shape[2]
        * f.shape[3]
        * lax.axis_size("gx")
        * lax.axis_size("gy")
        * lax.axis_size("gz")
    )
    diff_rho = rho_b - rho_a
    diff_x = jxb - jxa
    diff_y = jyb - jya
    diff_z = jzb - jza
    local_terms = (
        jnp.sum(diff_rho * diff_rho),
        jnp.sum(diff_x * diff_x + diff_y * diff_y + diff_z * diff_z),
        jnp.sum(jxb),
        jnp.sum(jyb),
        jnp.sum(jzb),
        jnp.sum(diff_x),
        jnp.sum(diff_y),
        jnp.sum(diff_z),
        jnp.sum(jxb * jxb + jyb * jyb + jzb * jzb),
        jnp.sum(jxb * diff_x + jyb * diff_y + jzb * diff_z),
    )
    (
        change_rho,
        change_mom,
        base_x,
        base_y,
        base_z,
        delta_x,
        delta_y,
        delta_z,
        energy_base,
        energy_cross,
    ) = lax.psum(
        (
            local_terms[0],
            local_terms[1],
            local_terms[2],
            local_terms[3],
            local_terms[4],
            local_terms[5],
            local_terms[6],
            local_terms[7],
            local_terms[8],
            local_terms[9],
        ),
        ("gx", "gy", "gz"),
    )
    change = (change_rho + change_mom) / cells
    gain = JUMP / (1.0 + limiter * change)
    jxp = jxb + gain * diff_x
    jyp = jyb + gain * diff_y
    jzp = jzb + gain * diff_z
    sum_x = base_x + gain * delta_x
    sum_y = base_y + gain * delta_y
    sum_z = base_z + gain * delta_z
    energy = energy_base + 2.0 * gain * energy_cross + gain * gain * change_mom
    rho_p = rho_b + gain * diff_rho
    lifted = equilibrium(rho_p, jxp, jyp, jzp)
    diagnostics = jnp.stack([change, sum_x / cells, sum_y / cells, sum_z / cells, energy / cells])
    return (lifted, diagnostics)


def solution(mesh):
    in_specs = (P(None, "gz", "gx", "gy"), P("gz", "gx", "gy"), P("gz", "gx", "gy"))
    out_specs = (P(None, "gz", "gx", "gy"), P())
    return jax.shard_map(
        per_device, mesh=mesh, in_specs=in_specs, out_specs=out_specs, check_vma=False
    )
```

profile of v0, /device:TPU:0, one launch (start us, length us, event | category | flops | bytes accessed | tf_op | source)
XLA Modules:
  0.0 191.6 jit_solution(2588128891063399128)
XLA Ops:
  5.4 5.1 %collective-permute-start = (f32[19,8,1,128]{3,2,1,0:T(1,128)S(1)}, f32[19,8,1,128]{3,2,1,0:T(1,128)S(1)}, u32[]{:S(2)}, u32[]{:S(2)}) collective-permute-start(f32[19,8,1,128]{3,2,1,0:T(1,128)S(1)} %get-tuple-element.152), channel_id=1, source_target_pairs={{8,0},{16,8},{24,16},{0,24},{9,1},{17,9},{25,17},{1,25},{10,2},{18... | collective-permute-start | bytes 233480 | tf_op jit(solution)/shard_map/ppermute | solution.py:44
  10.5 2.4 %collective-permute-done = f32[19,8,1,128]{3,2,1,0:T(1,128)S(1)} collective-permute-done((f32[19,8,1,128]{3,2,1,0:T(1,128)S(1)}, f32[19,8,1,128]{3,2,1,0:T(1,128)S(1)}, u32[]{:S(2)}, u32[]{:S(2)}) %collective-permute-start) | collective-permute-done | bytes 77856 | tf_op jit(solution)/shard_map/ppermute | solution.py:44
  13.0 3.7 %collective-permute-done.1 = f32[19,8,1,128]{3,2,1,0:T(1,128)S(1)} collective-permute-done((f32[19,8,1,128]{3,2,1,0:T(1,128)S(1)}, f32[19,8,1,128]{3,2,1,0:T(1,128)S(1)}, u32[]{:S(2)}, u32[]{:S(2)}) %collective-permute-start.1) | collective-permute-done | bytes 77856 | tf_op jit(solution)/shard_map/ppermute | solution.py:43
  24.1 1.6 collective-permute-start.4
  26.3 8.1 %collective-permute-done.4 = f32[19,1,10,130]{3,2,1,0:T(8,128)S(1)} collective-permute-done((f32[19,1,10,130]{3,2,1,0:T(8,128)S(1)}, f32[19,1,10,130]{3,2,1,0:T(8,128)S(1)}, u32[]{:S(2)}, u32[]{:S(2)}) %collective-permute-start.4) | collective-permute-done | bytes 98832 | tf_op jit(solution)/shard_map/ppermute | solution.py:44
  34.4 6.2 %collective-permute-done.5 = f32[19,1,10,130]{3,2,1,0:T(8,128)S(1)} collective-permute-done((f32[19,1,10,130]{3,2,1,0:T(8,128)S(1)}, f32[19,1,10,130]{3,2,1,0:T(8,128)S(1)}, u32[]{:S(2)}, u32[]{:S(2)}) %collective-permute-start.5) | collective-permute-done | bytes 98832 | tf_op jit(solution)/shard_map/ppermute | solution.py:43
  44.3 2.4 %collective-permute-done.6 = f32[19,8,1,128]{3,2,1,0:T(1,128)S(1)} collective-permute-done((f32[19,8,1,128]{3,2,1,0:T(1,128)S(1)}, f32[19,8,1,128]{3,2,1,0:T(1,128)S(1)}, u32[]{:S(2)}, u32[]{:S(2)}) %collective-permute-start.6) | collective-permute-done | bytes 77856 | tf_op jit(solution)/shard_map/ppermute | solution.py:44
  46.7 2.3 %collective-permute-done.7 = f32[19,8,1,128]{3,2,1,0:T(1,128)S(1)} collective-permute-done((f32[19,8,1,128]{3,2,1,0:T(1,128)S(1)}, f32[19,8,1,128]{3,2,1,0:T(1,128)S(1)}, u32[]{:S(2)}, u32[]{:S(2)}) %collective-permute-start.7) | collective-permute-done | bytes 77856 | tf_op jit(solution)/shard_map/ppermute | solution.py:43
  56.6 1.6 collective-permute-start.10
  58.8 8.1 %collective-permute-done.10 = f32[19,1,10,130]{3,2,1,0:T(8,128)S(1)} collective-permute-done((f32[19,1,10,130]{3,2,1,0:T(8,128)S(1)}, f32[19,1,10,130]{3,2,1,0:T(8,128)S(1)}, u32[]{:S(2)}, u32[]{:S(2)}) %collective-permute-start.10) | collective-permute-done | bytes 98832 | tf_op jit(solution)/shard_map/ppermute | solution.py:44
  66.9 5.1 %collective-permute-done.11 = f32[19,1,10,130]{3,2,1,0:T(8,128)S(1)} collective-permute-done((f32[19,1,10,130]{3,2,1,0:T(8,128)S(1)}, f32[19,1,10,130]{3,2,1,0:T(8,128)S(1)}, u32[]{:S(2)}, u32[]{:S(2)}) %collective-permute-start.11) | collective-permute-done | bytes 98832 | tf_op jit(solution)/shard_map/ppermute | solution.py:43
  73.8 1.9 %collective-permute-start.13 = (f32[19,8,1,128]{3,2,1,0:T(1,128)S(1)}, f32[19,8,1,128]{3,2,1,0:T(1,128)S(1)}, u32[]{:S(2)}, u32[]{:S(2)}) collective-permute-start(f32[19,8,1,128]{3,2,1,0:T(1,128)S(1)} %get-tuple-element.147), channel_id=1, source_target_pairs={{0,8},{8,16},{16,24},{24,0},{1,9},{9,17},{17,25},{25,1},{2,10},{10... | collective-permute-start | bytes 233480 | tf_op jit(solution)/shard_map/ppermute | solution.py:43
  75.7 2.7 %collective-permute-done.12 = f32[19,8,1,128]{3,2,1,0:T(1,128)S(1)} collective-permute-done((f32[19,8,1,128]{3,2,1,0:T(1,128)S(1)}, f32[19,8,1,128]{3,2,1,0:T(1,128)S(1)}, u32[]{:S(2)}, u32[]{:S(2)}) %collective-permute-start.12) | collective-permute-done | bytes 77856 | tf_op jit(solution)/shard_map/ppermute | solution.py:44
  84.4 1.6 collective-permute-done.15
  87.9 1.6 collective-permute-start.16
  90.1 8.1 %collective-permute-done.16 = f32[19,1,10,130]{3,2,1,0:T(8,128)S(1)} collective-permute-done((f32[19,1,10,130]{3,2,1,0:T(8,128)S(1)}, f32[19,1,10,130]{3,2,1,0:T(8,128)S(1)}, u32[]{:S(2)}, u32[]{:S(2)}) %collective-permute-start.16) | collective-permute-done | bytes 98832 | tf_op jit(solution)/shard_map/ppermute | solution.py:44
  98.2 6.4 %collective-permute-done.17 = f32[19,1,10,130]{3,2,1,0:T(8,128)S(1)} collective-permute-done((f32[19,1,10,130]{3,2,1,0:T(8,128)S(1)}, f32[19,1,10,130]{3,2,1,0:T(8,128)S(1)}, u32[]{:S(2)}, u32[]{:S(2)}) %collective-permute-start.17) | collective-permute-done | bytes 98832 | tf_op jit(solution)/shard_map/ppermute | solution.py:43
  106.9 3.8 %collective-permute-start.19 = (f32[19,8,1,128]{3,2,1,0:T(1,128)S(1)}, f32[19,8,1,128]{3,2,1,0:T(1,128)S(1)}, u32[]{:S(2)}, u32[]{:S(2)}) collective-permute-start(f32[19,8,1,128]{3,2,1,0:T(1,128)S(1)} %get-tuple-element.145), channel_id=1, source_target_pairs={{8,0},{16,8},{24,16},{0,24},{9,1},{17,9},{25,17},{1,25},{10,2},{18... | collective-permute-start | bytes 233480 | tf_op jit(solution)/shard_map/ppermute | solution.py:44
  110.7 2.9 %collective-permute-done.18 = f32[19,8,1,128]{3,2,1,0:T(1,128)S(1)} collective-permute-done((f32[19,8,1,128]{3,2,1,0:T(1,128)S(1)}, f32[19,8,1,128]{3,2,1,0:T(1,128)S(1)}, u32[]{:S(2)}, u32[]{:S(2)}) %collective-permute-start.18) | collective-permute-done | bytes 77856 | tf_op jit(solution)/shard_map/ppermute | solution.py:43
  116.3 1.8 collective-permute-start.21
  120.8 2.2 %copy.221 = f32[19,8,10,1]{3,2,1,0:T(8,128)S(1)} copy(f32[19,8,10,1]{0,1,3,2:T(8,128)} %collective-permute-done.21) | data formatting | bytes 12160 | tf_op jit(solution)/shard_map/ppermute | solution.py:44
  125.7 8.1 %collective-permute-done.22 = f32[19,1,10,130]{3,2,1,0:T(8,128)S(1)} collective-permute-done((f32[19,1,10,130]{3,2,1,0:T(8,128)S(1)}, f32[19,1,10,130]{3,2,1,0:T(8,128)S(1)}, u32[]{:S(2)}, u32[]{:S(2)}) %collective-permute-start.22) | collective-permute-done | bytes 98832 | tf_op jit(solution)/shard_map/ppermute | solution.py:43
  133.8 4.5 %collective-permute-done.23 = f32[19,1,10,130]{3,2,1,0:T(8,128)S(1)} collective-permute-done((f32[19,1,10,130]{3,2,1,0:T(8,128)S(1)}, f32[19,1,10,130]{3,2,1,0:T(8,128)S(1)}, u32[]{:S(2)}, u32[]{:S(2)}) %collective-permute-start.23) | collective-permute-done | bytes 98832 | tf_op jit(solution)/shard_map/ppermute | solution.py:44
  141.9 40.1 %all-reduce = (f32[]{:T(128)}, f32[]{:T(128)}, f32[]{:T(128)}, f32[]{:T(128)}, f32[]{:T(128)}, /*index=5*/f32[]{:T(128)}, f32[]{:T(128)}, f32[]{:T(128)}, f32[]{:T(128)}, f32[]{:T(128)}) all-reduce(f32[]{:T(128)} %fusion.287, f32[]{:T(128)} %get-tuple-element.5, ...), channel_id=1, replica_groups=mesh['gx'=4,'gy'=4,'gz'=2] {'gx','gy','gz'}, use_global_device_ids=true, to_apply=%region_2.3 | all-reduce | flops 10 | bytes 80 | tf_op jit(solution)/shard_map/psum | solution.py:144
  (381 shorter events, 49.2 us)
Async XLA Ops:
  5.4 7.6 %collective-permute-start = (f32[19,8,1,128]{3,2,1,0:T(1,128)S(1)}, f32[19,8,1,128]{3,2,1,0:T(1,128)S(1)}, u32[]{:S(2)}, u32[]{:S(2)}) collective-permute-start(f32[19,8,1,128]{3,2,1,0:T(1,128)S(1)} %get-tuple-element.152), channel_id=1, source_target_pairs={{8,0},{16,8},{24,16},{0,24},{9,1},{17,9},{25,17},{1,25},{10,2},{18... | collective-permute-start | bytes 233480 | tf_op jit(solution)/shard_map/ppermute | solution.py:44
  10.5 6.2 %collective-permute-start.1 = (f32[19,8,1,128]{3,2,1,0:T(1,128)S(1)}, f32[19,8,1,128]{3,2,1,0:T(1,128)S(1)}, u32[]{:S(2)}, u32[]{:S(2)}) collective-permute-start(f32[19,8,1,128]{3,2,1,0:T(1,128)S(1)} %get-tuple-element.151), channel_id=1, source_target_pairs={{0,8},{8,16},{16,24},{24,0},{1,9},{9,17},{17,25},{25,1},{2,10},{10... | collective-permute-start | bytes 233480 | tf_op jit(solution)/shard_map/ppermute | solution.py:43
  18.1 1.7 collective-permute-start.2
  18.8 3.5 %collective-permute-start.3 = (f32[19,8,10,1]{0,1,3,2:T(8,128)S(1)}, f32[19,8,10,1]{0,1,3,2:T(8,128)S(1)}, u32[]{:S(2)}, u32[]{:S(2)}) collective-permute-start(f32[19,8,10,1]{0,1,3,2:T(8,128)S(1)} %copy.202), channel_id=1, source_target_pairs={{0,2},{2,4},{4,6},{6,0},{1,3},{3,5},{5,7},{7,1},{8,10},{10,12},{12... | collective-permute-start | bytes 18248 | tf_op jit(solution)/shard_map/ppermute | solution.py:43
  24.1 10.3 %collective-permute-start.4 = (f32[19,1,10,130]{3,2,1,0:T(8,128)S(1)}, f32[19,1,10,130]{3,2,1,0:T(8,128)S(1)}, u32[]{:S(2)}, u32[]{:S(2)}) collective-permute-start(f32[19,1,10,130]{3,2,1,0:T(8,128)S(1)} %get-tuple-element.136), channel_id=1, source_target_pairs={{1,0},{0,1},{3,2},{2,3},{5,4},{4,5},{7,6},{6,7},{9,8},{8,9},{11,10... | collective-permute-start | bytes 296408 | tf_op jit(solution)/shard_map/ppermute | solution.py:44
  25.7 14.9 %collective-permute-start.5 = (f32[19,1,10,130]{3,2,1,0:T(8,128)S(1)}, f32[19,1,10,130]{3,2,1,0:T(8,128)S(1)}, u32[]{:S(2)}, u32[]{:S(2)}) collective-permute-start(f32[19,1,10,130]{3,2,1,0:T(8,128)S(1)} %get-tuple-element.135), channel_id=1, source_target_pairs={{0,1},{1,0},{2,3},{3,2},{4,5},{5,4},{6,7},{7,6},{8,9},{9,8},{10,11... | collective-permute-start | bytes 296408 | tf_op jit(solution)/shard_map/ppermute | solution.py:43
  42.2 4.5 %collective-permute-start.6 = (f32[19,8,1,128]{3,2,1,0:T(1,128)S(1)}, f32[19,8,1,128]{3,2,1,0:T(1,128)S(1)}, u32[]{:S(2)}, u32[]{:S(2)}) collective-permute-start(f32[19,8,1,128]{3,2,1,0:T(1,128)S(1)} %get-tuple-element.150), channel_id=1, source_target_pairs={{8,0},{16,8},{24,16},{0,24},{9,1},{17,9},{25,17},{1,25},{10,2},{18... | collective-permute-start | bytes 233480 | tf_op jit(solution)/shard_map/ppermute | solution.py:44
  42.8 6.2 %collective-permute-start.7 = (f32[19,8,1,128]{3,2,1,0:T(1,128)S(1)}, f32[19,8,1,128]{3,2,1,0:T(1,128)S(1)}, u32[]{:S(2)}, u32[]{:S(2)}) collective-permute-start(f32[19,8,1,128]{3,2,1,0:T(1,128)S(1)} %get-tuple-element.149), channel_id=1, source_target_pairs={{0,8},{8,16},{16,24},{24,0},{1,9},{9,17},{17,25},{25,1},{2,10},{10... | collective-permute-start | bytes 233480 | tf_op jit(solution)/shard_map/ppermute | solution.py:43
  50.4 1.7 collective-permute-start.8
  51.1 3.6 %collective-permute-start.9 = (f32[19,8,10,1]{0,1,3,2:T(8,128)S(1)}, f32[19,8,10,1]{0,1,3,2:T(8,128)S(1)}, u32[]{:S(2)}, u32[]{:S(2)}) collective-permute-start(f32[19,8,10,1]{0,1,3,2:T(8,128)S(1)} %copy.208), channel_id=1, source_target_pairs={{0,2},{2,4},{4,6},{6,0},{1,3},{3,5},{5,7},{7,1},{8,10},{10,12},{12... | collective-permute-start | bytes 18248 | tf_op jit(solution)/shard_map/ppermute | solution.py:43
  56.6 10.3 %collective-permute-start.10 = (f32[19,1,10,130]{3,2,1,0:T(8,128)S(1)}, f32[19,1,10,130]{3,2,1,0:T(8,128)S(1)}, u32[]{:S(2)}, u32[]{:S(2)}) collective-permute-start(f32[19,1,10,130]{3,2,1,0:T(8,128)S(1)} %get-tuple-element.134), channel_id=1, source_target_pairs={{1,0},{0,1},{3,2},{2,3},{5,4},{4,5},{7,6},{6,7},{9,8},{8,9},{11,10... | collective-permute-start | bytes 296408 | tf_op jit(solution)/shard_map/ppermute | solution.py:44
  58.2 13.8 %collective-permute-start.11 = (f32[19,1,10,130]{3,2,1,0:T(8,128)S(1)}, f32[19,1,10,130]{3,2,1,0:T(8,128)S(1)}, u32[]{:S(2)}, u32[]{:S(2)}) collective-permute-start(f32[19,1,10,130]{3,2,1,0:T(8,128)S(1)} %get-tuple-element.133), channel_id=1, source_target_pairs={{0,1},{1,0},{2,3},{3,2},{4,5},{5,4},{6,7},{7,6},{8,9},{9,8},{10,11... | collective-permute-start | bytes 296408 | tf_op jit(solution)/shard_map/ppermute | solution.py:43
  73.6 4.8 %collective-permute-start.12 = (f32[19,8,1,128]{3,2,1,0:T(1,128)S(1)}, f32[19,8,1,128]{3,2,1,0:T(1,128)S(1)}, u32[]{:S(2)}, u32[]{:S(2)}) collective-permute-start(f32[19,8,1,128]{3,2,1,0:T(1,128)S(1)} %get-tuple-element.148), channel_id=1, source_target_pairs={{8,0},{16,8},{24,16},{0,24},{9,1},{17,9},{25,17},{1,25},{10,2},{18... | collective-permute-start | bytes 233480 | tf_op jit(solution)/shard_map/ppermute | solution.py:44
  73.8 6.2 %collective-permute-start.13 = (f32[19,8,1,128]{3,2,1,0:T(1,128)S(1)}, f32[19,8,1,128]{3,2,1,0:T(1,128)S(1)}, u32[]{:S(2)}, u32[]{:S(2)}) collective-permute-start(f32[19,8,1,128]{3,2,1,0:T(1,128)S(1)} %get-tuple-element.147), channel_id=1, source_target_pairs={{0,8},{8,16},{16,24},{24,0},{1,9},{9,17},{17,25},{25,1},{2,10},{10... | collective-permute-start | bytes 233480 | tf_op jit(solution)/shard_map/ppermute | solution.py:43
  81.3 1.7 collective-permute-start.14
  82.1 3.9 %collective-permute-start.15 = (f32[19,8,10,1]{0,1,3,2:T(8,128)S(1)}, f32[19,8,10,1]{0,1,3,2:T(8,128)S(1)}, u32[]{:S(2)}, u32[]{:S(2)}) collective-permute-start(f32[19,8,10,1]{0,1,3,2:T(8,128)S(1)} %copy.214), channel_id=1, source_target_pairs={{0,2},{2,4},{4,6},{6,0},{1,3},{3,5},{5,7},{7,1},{8,10},{10,12},{12... | collective-permute-start | bytes 18248 | tf_op jit(solution)/shard_map/ppermute | solution.py:43
  87.9 10.3 %collective-permute-start.16 = (f32[19,1,10,130]{3,2,1,0:T(8,128)S(1)}, f32[19,1,10,130]{3,2,1,0:T(8,128)S(1)}, u32[]{:S(2)}, u32[]{:S(2)}) collective-permute-start(f32[19,1,10,130]{3,2,1,0:T(8,128)S(1)} %get-tuple-element.132), channel_id=1, source_target_pairs={{1,0},{0,1},{3,2},{2,3},{5,4},{4,5},{7,6},{6,7},{9,8},{8,9},{11,10... | collective-permute-start | bytes 296408 | tf_op jit(solution)/shard_map/ppermute | solution.py:44
  89.5 15.1 %collective-permute-start.17 = (f32[19,1,10,130]{3,2,1,0:T(8,128)S(1)}, f32[19,1,10,130]{3,2,1,0:T(8,128)S(1)}, u32[]{:S(2)}, u32[]{:S(2)}) collective-permute-start(f32[19,1,10,130]{3,2,1,0:T(8,128)S(1)} %get-tuple-element.131), channel_id=1, source_target_pairs={{0,1},{1,0},{2,3},{3,2},{4,5},{5,4},{6,7},{7,6},{8,9},{9,8},{10,11... | collective-permute-start | bytes 296408 | tf_op jit(solution)/shard_map/ppermute | solution.py:43
  106.8 6.7 %collective-permute-start.18 = (f32[19,8,1,128]{3,2,1,0:T(1,128)S(1)}, f32[19,8,1,128]{3,2,1,0:T(1,128)S(1)}, u32[]{:S(2)}, u32[]{:S(2)}) collective-permute-start(f32[19,8,1,128]{3,2,1,0:T(1,128)S(1)} %get-tuple-element.146), channel_id=1, source_target_pairs={{0,8},{8,16},{16,24},{24,0},{1,9},{9,17},{17,25},{25,1},{2,10},{10... | collective-permute-start | bytes 233480 | tf_op jit(solution)/shard_map/ppermute | solution.py:43
  106.9 6.7 %collective-permute-start.19 = (f32[19,8,1,128]{3,2,1,0:T(1,128)S(1)}, f32[19,8,1,128]{3,2,1,0:T(1,128)S(1)}, u32[]{:S(2)}, u32[]{:S(2)}) collective-permute-start(f32[19,8,1,128]{3,2,1,0:T(1,128)S(1)} %get-tuple-element.145), channel_id=1, source_target_pairs={{8,0},{16,8},{24,16},{0,24},{9,1},{17,9},{25,17},{1,25},{10,2},{18... | collective-permute-start | bytes 233480 | tf_op jit(solution)/shard_map/ppermute | solution.py:44
  115.6 3.9 %collective-permute-start.20 = (f32[19,8,10,1]{0,1,3,2:T(8,128)}, f32[19,8,10,1]{0,1,3,2:T(8,128)S(1)}, u32[]{:S(2)}, u32[]{:S(2)}) collective-permute-start(f32[19,8,10,1]{0,1,3,2:T(8,128)} %copy.218), channel_id=1, source_target_pairs={{0,2},{2,4},{4,6},{6,0},{1,3},{3,5},{5,7},{7,1},{8,10},{10,12},{12... | collective-permute-start | bytes 18248 | tf_op jit(solution)/shard_map/ppermute | solution.py:43
  116.3 4.5 %collective-permute-start.21 = (f32[19,8,10,1]{0,1,3,2:T(8,128)S(1)}, f32[19,8,10,1]{0,1,3,2:T(8,128)}, u32[]{:S(2)}, u32[]{:S(2)}) collective-permute-start(f32[19,8,10,1]{0,1,3,2:T(8,128)S(1)} %copy.220), channel_id=1, source_target_pairs={{2,0},{4,2},{6,4},{0,6},{3,1},{5,3},{7,5},{1,7},{10,8},{12,10},{14... | collective-permute-start | bytes 18248 | tf_op jit(solution)/shard_map/ppermute | solution.py:44
  123.5 10.3 %collective-permute-start.22 = (f32[19,1,10,130]{3,2,1,0:T(8,128)S(1)}, f32[19,1,10,130]{3,2,1,0:T(8,128)S(1)}, u32[]{:S(2)}, u32[]{:S(2)}) collective-permute-start(f32[19,1,10,130]{3,2,1,0:T(8,128)S(1)} %get-tuple-element.129), channel_id=1, source_target_pairs={{0,1},{1,0},{2,3},{3,2},{4,5},{5,4},{6,7},{7,6},{8,9},{9,8},{10,11... | collective-permute-start | bytes 296408 | tf_op jit(solution)/shard_map/ppermute | solution.py:43
  125.1 13.1 %collective-permute-start.23 = (f32[19,1,10,130]{3,2,1,0:T(8,128)S(1)}, f32[19,1,10,130]{3,2,1,0:T(8,128)S(1)}, u32[]{:S(2)}, u32[]{:S(2)}) collective-permute-start(f32[19,1,10,130]{3,2,1,0:T(8,128)S(1)} %get-tuple-element.130), channel_id=1, source_target_pairs={{1,0},{0,1},{3,2},{2,3},{5,4},{4,5},{7,6},{6,7},{9,8},{8,9},{11,10... | collective-permute-start | bytes 296408 | tf_op jit(solution)/shard_map/ppermute | solution.py:44
  (56 other events, 307.0 us)
where the time goes:
time: 193 us; the launch traced here: 192 us
  waiting for transfers between devices  79.2 us (41%)
  blocking collectives  40.1 us (21%)
  starting transfers between devices  25.2 us (13%)
  local copies, waits for them, and re-layouts  23.9 us (12%)
  other arithmetic  13.1 us (7%)
  between operations  9.95 us (5%)
    ppermute x12, waiting for transfers between devices, extended(): before = lax.ppermute(last, axis, up)  41.7 us
    psum x1, blocking collectives, per_device(): lax.psum((local_terms[0], local_terms[1], local_terms[2], local_terms[3],...  40.1 us
    ppermute x12, waiting for transfers between devices, extended(): after = lax.ppermute(first, axis, down)  37.6 us
    ppermute x12, starting transfers between devices, extended(): after = lax.ppermute(first, axis, down)  16.9 us
    ppermute x12, starting transfers between devices, extended(): before = lax.ppermute(last, axis, up)  8.35 us
    ppermute x4, local copies, waits for them, and re-layouts, extended(): after = lax.ppermute(first, axis, down)  6.25 us
    unnamed x90, other arithmetic  5.58 us
    ppermute x4, local copies, waits for them, and re-layouts, extended(): before = lax.ppermute(last, axis, up)  5.46 us
  transfers between devices with their start and end apart: 24, of which 22 were waited for; matrix products, arithmetic and copies ran while one was open for 4% of the time, Pallas kernels for 0%

commit v1 on v0

v1 whole, which is shorter than its diff:
```python
import functools

import jax
import jax.numpy as jnp
from jax import lax
from jax.experimental import pallas as pl
from jax.experimental.pallas import tpu as pltpu
from jax.sharding import PartitionSpec as P

STEPS = 4
JUMP = 2
LIMITER = 25.0
AXES = ("gx", "gy", "gz")

LATTICE = [
    (0, 0, 0),
    (1, 0, 0), (-1, 0, 0), (0, 1, 0), (0, -1, 0), (0, 0, 1), (0, 0, -1),
    (1, 1, 0), (-1, -1, 0), (1, -1, 0), (-1, 1, 0),
    (1, 0, 1), (-1, 0, -1), (1, 0, -1), (-1, 0, 1),
    (0, 1, 1), (0, -1, -1), (0, 1, -1), (0, -1, 1),
]
WEIGHTS = [1.0 / 3.0] + [1.0 / 18.0] * 6 + [1.0 / 36.0] * 12
CROSS = [[[i for i in range(19) if LATTICE[i][axis] == sign] for sign in (1, -1)] for axis in range(3)]
ORDER = [i for i in range(19) if LATTICE[i][2] == 0] + CROSS[2][0] + CROSS[2][1]
SLOT = {i: ORDER.index(i) for i in range(19)}
INDEX = {v: i for i, v in enumerate(LATTICE)}


def side(c):
    return 0 if c == 1 else 1


def rank_in(axis, i):
    return CROSS[axis][side(LATTICE[i][axis])].index(i)


def moments(f):
    def total(terms):
        terms = list(terms)
        while len(terms) > 1:
            terms = [terms[j] + terms[j + 1] if j + 1 < len(terms) else terms[j] for j in range(0, len(terms), 2)]
        return terms[0]

    comps = []
    for axis in range(3):
        comps.append(total(f[p] - f[p + 1] for p in range(1, 19, 2) if LATTICE[p][axis] == 1)
                     + 0.0)
    for axis in range(3):
        extra = [f[p] - f[p + 1] for p in range(1, 19, 2) if LATTICE[p][axis] == -1]
        if extra:
            comps[axis] = comps[axis] - total(extra)
    return total(f), comps[0], comps[1], comps[2]


def equilibrium_parts(rho, jx, jy, jz):
    inverse = 3.0 / jnp.maximum(rho, 0.5)
    v = (jx * inverse, jy * inverse, jz * inverse)
    base = 1.0 - (v[0] * v[0] + v[1] * v[1] + v[2] * v[2]) * (1.5 / 9.0)
    return v, base


def projected(v, i):
    out = None
    for comp, vel in zip(LATTICE[i], v):
        if comp == 1:
            out = vel if out is None else out + vel
        elif comp == -1:
            out = -vel if out is None else out - vel
    return out


def collide(f, omega, solid):
    rho, jx, jy, jz = moments(f)
    v, base = equilibrium_parts(rho, jx, jy, jz)
    keep = 1.0 - omega
    scale = omega * rho
    scaled = {w: scale * w for w in set(WEIGHTS)}
    post = [None] * 19
    post[0] = jnp.where(solid, f[0], keep * f[0] + scaled[WEIGHTS[0]] * base)
    for i in range(1, 19, 2):
        p = projected(v, i)
        even = base + 0.5 * (p * p)
        w = scaled[WEIGHTS[i]]
        post[i] = jnp.where(solid, f[i + 1], keep * f[i] + w * (even + p))
        post[i + 1] = jnp.where(solid, f[i], keep * f[i + 1] + w * (even - p))
    return post


def kernel(sizes, cells, pop_hbm, omega_hbm, obstacle_hbm, lifted_ref, diag_ref,
           f_in, om, ob, post, xs, ys, es, hx, hy, hz, hxy, hyz, hxz, cs, before, after, gather,
           load_sem, send_sem, recv_sem, gsend_sem, grecv_sem):
    Z, X, Y = om.shape
    nx, ny, nz = (sizes[a] for a in AXES)
    n = nx * ny * nz
    me = tuple(lax.axis_index(a) for a in AXES)

    def device(offset):
        return {a: lax.rem(me[d] + (offset[d] % sizes[a]), sizes[a]) for d, a in enumerate(AXES)}

    loads = []
    for z in range(Z):
        loads.append(pltpu.make_async_copy(pop_hbm.at[:, z], f_in.at[:, z], load_sem.at[z]))
    loads.append(pltpu.make_async_copy(omega_hbm, om, load_sem.at[Z]))
    loads.append(pltpu.make_async_copy(obstacle_hbm, ob, load_sem.at[Z + 1]))
    for copy in loads[::-1]:
        copy.start()

    far = (nx // 2, ny // 2, nz // 2)
    covered = max(max(far), (sum(far) + 1) // 2) <= STEPS
    wrapped = lambda c: (c[0] % nx, c[1] % ny, c[2] % nz)
    everyone = [(k // (ny * nz), k // nz % ny, k % nz) for k in range(1, n)]
    greet = sorted({wrapped(c) for c in LATTICE} - {(0, 0, 0)}) if covered else everyone
    barrier = pltpu.get_barrier_semaphore()
    for offset in greet:
        pl.semaphore_signal(barrier, inc=1, device_id=device(offset), device_id_type=pl.DeviceIdType.MESH)

    lane = lax.broadcasted_iota(jnp.int32, (X, Y), 1)
    row = lax.broadcasted_iota(jnp.int32, (X, Y), 0)
    zrow = lax.broadcasted_iota(jnp.int32, (Z, Y), 0)
    zlane = lax.broadcasted_iota(jnp.int32, (Z, Y), 1)
    zsides = (1,) if nz == 2 else (1, -1)
    zside = lambda c: 0 if nz == 2 else side(c)

    def messages(s):
        out = []
        for c in (1, -1):
            d = side(c)
            out.append(((0, 0, c), post.at[s, pl.ds(9 + 5 * d, 5), Z - 1 if c == 1 else 0], hz.at[s, d]))
            out.append(((c, 0, 0), xs.at[s, d], hx.at[s, d]))
            out.append(((0, c, 0), ys.at[s, d], hy.at[s, d]))
            for b in (1, -1):
                k = rank_in(0, INDEX[(c, b, 0)])
                out.append(((c, b, 0), xs.at[s, d, k], hxy.at[s, d, side(b)]))
            for b in zsides:
                out.append(((0, c, b), ys.at[s, d], hyz.at[s, d, zside(b)]))
                out.append(((c, 0, b), es.at[s, d], hxz.at[s, d, zside(b)]))
        return [
            pltpu.make_async_remote_copy(
                src_ref=src, dst_ref=dst, send_sem=send_sem.at[s, m], recv_sem=recv_sem.at[s, m],
                device_id=device(offset), device_id_type=pl.DeviceIdType.MESH)
            for m, (offset, src, dst) in enumerate(out)
        ]

    def pack(s):
        for d in (0, 1):
            edge = X - 1 if d == 0 else 0
            for k, i in enumerate(CROSS[0][d]):
                xs[s, d, k] = post[s, SLOT[i], :, edge, :]
            up = rank_in(0, INDEX[(1 - 2 * d, 0, 1)])
            down = rank_in(0, INDEX[(1 - 2 * d, 0, -1)])
            first = post[s, SLOT[INDEX[(1 - 2 * d, 0, 1)]], Z - 1, edge:edge + 1, :]
            second = post[s, SLOT[INDEX[(1 - 2 * d, 0, -1)]], 0, edge:edge + 1, :]
            es[s, d] = jnp.where(row == 0, jnp.broadcast_to(first, (X, Y)), jnp.broadcast_to(second, (X, Y)))
        for d in (0, 1):
            edge = Y - 1 if d == 0 else 0
            tile = jnp.zeros((X, Y), jnp.float32)
            for k, i in enumerate(CROSS[1][d]):
                for z in range(Z):
                    m = k * Z + z
                    moved = pltpu.roll(post[s, SLOT[i], z], (m - edge) % Y, 1)
                    tile = jnp.where(lane == m, moved, tile)
            ys[s, d] = tile

    def columns(s):
        for d in (0, 1):
            for k, i in enumerate(CROSS[0][d]):
                cx, cy, cz = LATTICE[i]
                col = hx[s, d, k]
                if cy:
                    edge = 0 if cy == 1 else Y - 1
                    corner = pltpu.roll(hxy[s, d, side(cy)], cy % Y, 1)
                    col = jnp.where(zlane == edge, corner, pltpu.roll(col, cy % Y, 1))
                if cz:
                    edge = 0 if cz == 1 else Z - 1
                    r = 0 if cz == 1 else 1
                    corner = jnp.broadcast_to(hxz[s, d, zside(cz), r:r + 1, :], (Z, Y))
                    col = jnp.where(zrow == edge, corner, pltpu.roll(col, cz % Z, 0))
                cs[s, d, k] = col

    def streamed(s, z):
        out = []
        for i in range(19):
            cx, cy, cz = LATTICE[i]
            zs = z - cz
            inside = 0 <= zs < Z
            tile = post[s, SLOT[i], zs] if inside else hz[s, side(cz), rank_in(2, i)]
            if cy:
                source = hy[s, side(cy)] if inside else hyz[s, side(cy), zside(cz)]
                m = rank_in(1, i) * Z + zs % Z
                edge = 0 if cy == 1 else Y - 1
                tile = jnp.where(lane == edge, pltpu.roll(source, (edge - m) % Y, 1), pltpu.roll(tile, cy % Y, 1))
            if cx:
                edge = 0 if cx == 1 else X - 1
                col = jnp.broadcast_to(cs[s, side(cx), rank_in(0, i), z:z + 1, :], (X, Y))
                tile = jnp.where(row == edge, col, pltpu.roll(tile, cx % X, 0))
            out.append(tile)
        return out

    sent = []
    loads[Z].wait()
    loads[Z + 1].wait()
    for s in range(STEPS):
        if s:
            columns(s - 1)
        for z in range(Z):
            if s == 0:
                loads[z].wait()
                f = [f_in[i, z] for i in range(19)]
            else:
                f = streamed(s - 1, z)
            if s == STEPS - 1:
                for c, value in enumerate(moments(f)):
                    before[c, z] = value
            new = collide(f, om[z], ob[z] == 1)
            for i in range(19):
                post[s, SLOT[i], z] = new[i]
        pack(s)
        if s == 0:
            pl.semaphore_wait(barrier, len(greet))
        copies = messages(s)
        for copy in copies:
            copy.start()
        for copy in copies:
            copy.wait_recv()
        sent += copies

    columns(STEPS - 1)
    sums = [jnp.zeros((X, Y), jnp.float32) for _ in range(10)]
    for z in range(Z):
        b = moments(streamed(STEPS - 1, z))
        diff = []
        for c in range(4):
            after[c, z] = b[c]
            delta = b[c] - before[c, z]
            before[c, z] = delta
            diff.append(delta)
        change_mom = diff[1] * diff[1] + diff[2] * diff[2] + diff[3] * diff[3]
        terms = (diff[0] * diff[0], change_mom, b[1], b[2], b[3], diff[1], diff[2], diff[3],
                 b[1] * b[1] + b[2] * b[2] + b[3] * b[3],
                 b[1] * diff[1] + b[2] * diff[2] + b[3] * diff[3])
        sums = [a + t for a, t in zip(sums, terms)]
    wide = lax.broadcasted_iota(jnp.int32, (1, Y), 1)
    mine = jnp.zeros((1, Y), jnp.float32)
    for k, tile in enumerate(sums):
        whole = jnp.sum(jnp.sum(tile, axis=0, keepdims=True), axis=1, keepdims=True)
        mine = jnp.where(wide == k, whole, mine)
    slot = (me[0] * ny + me[1]) * nz + me[2]
    gather[slot] = mine
    stat = []
    for k, offset in enumerate(everyone):
        stat.append(pltpu.make_async_remote_copy(
            src_ref=gather.at[slot], dst_ref=gather.at[slot], send_sem=gsend_sem.at[k], recv_sem=grecv_sem.at[k],
            device_id=device(offset), device_id_type=pl.DeviceIdType.MESH))
    for copy in stat:
        copy.start()
    for copy in sent:
        copy.wait_send()
    for copy in stat:
        copy.wait_recv()
    total = jnp.sum(gather[...], axis=0)
    pick = lambda k: jnp.sum(jnp.where(wide == k, total, 0.0), axis=1, keepdims=True)
    t = [pick(k) for k in range(10)]
    change = (t[0] + t[1]) / cells
    gain = JUMP / (1.0 + LIMITER * change)
    diag = [change] + [(t[2 + c] + gain * t[5 + c]) / cells for c in range(3)]
    diag.append((t[8] + 2.0 * gain * t[9] + gain * gain * t[1]) / cells)
    for k, value in enumerate(diag):
        diag_ref[k] = value[0, 0]
    spread = jnp.broadcast_to(gain, (X, Y))
    for z in range(Z):
        rho, jx, jy, jz = (after[c, z] + spread * before[c, z] for c in range(4))
        v, base = equilibrium_parts(rho, jx, jy, jz)
        scaled = {w: rho * w for w in set(WEIGHTS)}
        lifted_ref[0, z] = scaled[WEIGHTS[0]] * base
        for i in range(1, 19, 2):
            p = projected(v, i)
            even = base + 0.5 * (p * p)
            lifted_ref[i, z] = scaled[WEIGHTS[i]] * (even + p)
            lifted_ref[i + 1, z] = scaled[WEIGHTS[i]] * (even - p)
    for copy in stat:
        copy.wait_send()


def solution(mesh):
    sizes = {a: mesh.shape[a] for a in AXES}
    n = sizes["gx"] * sizes["gy"] * sizes["gz"]

    def per_device(populations, omega, obstacle):
        Z, X, Y = omega.shape
        S = STEPS
        nzs = 1 if sizes["gz"] == 2 else 2
        count = 10 + 4 * nzs
        f32 = lambda *shape: pltpu.VMEM(shape, jnp.float32)
        return pl.pallas_call(
            functools.partial(kernel, sizes, float(Z * X * Y * n)),
            out_shape=(jax.ShapeDtypeStruct(populations.shape, jnp.float32), jax.ShapeDtypeStruct((5,), jnp.float32)),
            in_specs=[pl.BlockSpec(memory_space=pl.ANY)] * 3,
            out_specs=(pl.BlockSpec(memory_space=pltpu.VMEM), pl.BlockSpec(memory_space=pltpu.SMEM)),
            scratch_shapes=[
                f32(19, Z, X, Y), f32(Z, X, Y), pltpu.VMEM((Z, X, Y), jnp.int32),
                f32(S, 19, Z, X, Y),
                f32(S, 2, 5, Z, Y), f32(S, 2, X, Y), f32(S, 2, X, Y),
                f32(S, 2, 5, Z, Y), f32(S, 2, X, Y), f32(S, 2, 5, X, Y),
                f32(S, 2, 2, Z, Y), f32(S, 2, nzs, X, Y), f32(S, 2, nzs, X, Y),
                f32(S, 2, 5, Z, Y), f32(4, Z, X, Y), f32(4, Z, X, Y), f32(n, 1, Y),
                pltpu.SemaphoreType.DMA((Z + 2,)),
                pltpu.SemaphoreType.DMA((S, count)), pltpu.SemaphoreType.DMA((S, count)),
                pltpu.SemaphoreType.DMA((n,)), pltpu.SemaphoreType.DMA((n,)),
            ],
            compiler_params=pltpu.CompilerParams(collective_id=0, has_side_effects=True),
        )(populations, omega, obstacle)

    spec = P("gz", "gx", "gy")
    return jax.shard_map(
        per_device, mesh=mesh, in_specs=(P(None, *spec), spec, spec),
        out_specs=(P(None, *spec), P()), check_vma=False)
```

time: 193 us -> 36.2 us (0.19)
  waiting for transfers between devices: 79.2 us -> 0 us
  blocking collectives: 40.1 us -> 0 us
  Pallas kernels: 0 us -> 32.9 us
  starting transfers between devices: 25.2 us -> 0 us
  local copies, waits for them, and re-layouts: 23.9 us -> 2.47 us
  other arithmetic: 13.1 us -> 0 us
  between operations: 9.95 us -> 0.65 us
    ppermute x24 -> x0, waiting for transfers between devices: 79.2 us -> none  [the longest x12 41.7 us: extended(): before = lax.ppermute(last, axis, up)]
    psum x1 -> x0, blocking collectives: 40.1 us -> none  [per_device(): lax.psum((local_terms[0], local_terms[1], local_terms[2], local_terms[3],...]
    pallas_call x0 -> x1, Pallas kernels: none -> 32.9 us  [per_device(): pl.pallas_call(functools.partial(kernel, sizes, float(Z * X * Y * n)), ou...]
    ppermute x24 -> x0, starting transfers between devices: 25.2 us -> none  [the longest x12 16.9 us: extended(): after = lax.ppermute(first, axis, down)]
    ppermute x8 -> x0, local copies, waits for them, and re-layouts: 11.7 us -> none  [the longest x4 6.25 us: extended(): after = lax.ppermute(first, axis, down)]
    slice x16 -> x0, local copies, waits for them, and re-layouts: 8.32 us -> none  [the longest x10 4.99 us: extended(): last = lax.slice_in_dim(x, length - width, length, axis=dim)]
    unnamed x90 -> x0, other arithmetic: 5.58 us -> none
    reduce_sum x3 -> x0, other arithmetic: 3.35 us -> none  [the longest x1 1.5 us: per_device(): jnp.sum(diff_rho * diff_rho)]
  transfers between devices with their start and end apart: 24 -> 0, of which waited for: 22 -> 0; matrix products, arithmetic and copies ran while one was open for 4% -> 0% of each run, Pallas kernels for 0% -> 0%
where the time goes in v1:
time: 36.2 us; the launch traced here: 36 us
  Pallas kernels  32.9 us (91%)
  local copies, waits for them, and re-layouts  2.47 us (7%)
  between operations  0.65 us (2%)
    pallas_call x1, Pallas kernels, per_device(): pl.pallas_call(functools.partial(kernel, sizes, float(Z * X * Y * n)), ou...  32.9 us
    unnamed x4, local copies, waits for them, and re-layouts  2.47 us

profile of v1, /device:TPU:0, one launch (start us, length us, event | category | flops | bytes accessed | tf_op | source)
XLA Modules:
  0.0 36.0 jit_solution(11938209584452637746)
XLA Ops:
  0.6 32.9 %shard_map.50 = (f32[19,8,8,128]{3,2,1,0:T(8,128)}, f32[5]{0:T(128)}) custom-call(f32[19,8,8,128]{3,2,1,0:T(8,128)} %pop_hbm.1, f32[8,8,128]{2,1,0:T(8,128)} %omega_hbm.1, s32[8,8,128]{2,1,0:T(8,128)} %obstacle_hbm.1), custom_call_target="tpu_custom_call" | custom-call | tf_op jit(solution)/shard_map/pallas_call | solution.py:294
  33.5 0.0 copy-start
  33.5 2.0 %copy.7 = f32[19,8,8,128]{3,2,1,0:T(8,128)} copy(f32[19,8,8,128]{3,2,1,0:T(8,128)} %get-tuple-element.4) | data formatting | bytes 1245184
  35.5 0.0 copy-done
  35.5 0.5 %copy.8 = f32[5]{0:T(128)} copy(f32[5]{0:T(128)S(1)} %copy-done) | data formatting | bytes 40
Async XLA Ops:
  33.5 2.0 %copy-start = (f32[5]{0:T(128)S(1)}, f32[5]{0:T(128)}, u32[]{:S(2)}) copy-start(f32[5]{0:T(128)} %get-tuple-element.5) | copy-start | bytes 64

commit v2 on v1

--- a/solution.py
+++ b/solution.py
@@ -86,9 +86,9 @@
     return post
 
 
-def kernel(sizes, cells, pop_hbm, omega_hbm, obstacle_hbm, lifted_ref, diag_ref,
+def kernel(sizes, pop_hbm, omega_hbm, obstacle_hbm, total_ref, after_hbm, change_hbm,
            f_in, om, ob, post, xs, ys, es, hx, hy, hz, hxy, hyz, hxz, cs, before, after, gather,
-           load_sem, send_sem, recv_sem, gsend_sem, grecv_sem):
+           load_sem, out_sem, send_sem, recv_sem, gsend_sem, grecv_sem):
     Z, X, Y = om.shape
     nx, ny, nz = (sizes[a] for a in AXES)
     n = nx * ny * nz
@@ -134,14 +134,18 @@
             for b in zsides:
                 out.append(((0, c, b), ys.at[s, d], hyz.at[s, d, zside(b)]))
                 out.append(((c, 0, b), es.at[s, d], hxz.at[s, d, zside(b)]))
-        return [
-            pltpu.make_async_remote_copy(
+        copies = [
+            (offset, pltpu.make_async_remote_copy(
                 src_ref=src, dst_ref=dst, send_sem=send_sem.at[s, m], recv_sem=recv_sem.at[s, m],
-                device_id=device(offset), device_id_type=pl.DeviceIdType.MESH)
+                device_id=device(offset), device_id_type=pl.DeviceIdType.MESH))
             for m, (offset, src, dst) in enumerate(out)
         ]
-
-    def pack(s):
+        along_x = [c for o, c in copies if o[0]]
+        along_z = [c for o, c in copies if not o[0] and not o[1]]
+        along_y = [c for o, c in copies if not o[0] and o[1]]
+        return along_x, along_z, along_y
+
+    def pack_x(s):
         for d in (0, 1):
             edge = X - 1 if d == 0 else 0
             for k, i in enumerate(CROSS[0][d]):
@@ -151,6 +155,8 @@
             first = post[s, SLOT[INDEX[(1 - 2 * d, 0, 1)]], Z - 1, edge:edge + 1, :]
             second = post[s, SLOT[INDEX[(1 - 2 * d, 0, -1)]], 0, edge:edge + 1, :]
             es[s, d] = jnp.where(row == 0, jnp.broadcast_to(first, (X, Y)), jnp.broadcast_to(second, (X, Y)))
+
+    def pack_y(s):
         for d in (0, 1):
             edge = Y - 1 if d == 0 else 0
             tile = jnp.zeros((X, Y), jnp.float32)
@@ -214,12 +220,16 @@
             new = collide(f, om[z], ob[z] == 1)
             for i in range(19):
                 post[s, SLOT[i], z] = new[i]
-        pack(s)
+        along_x, along_z, along_y = messages(s)
+        pack_x(s)
         if s == 0:
             pl.semaphore_wait(barrier, len(greet))
-        copies = messages(s)
-        for copy in copies:
+        for copy in along_x + along_z:
             copy.start()
+        pack_y(s)
+        for copy in along_y:
+            copy.start()
+        copies = along_y + along_z + along_x
         for copy in copies:
             copy.wait_recv()
         sent += copies
@@ -253,11 +263,25 @@
             device_id=device(offset), device_id_type=pl.DeviceIdType.MESH))
     for copy in stat:
         copy.start()
+    out = [pltpu.make_async_copy(after, after_hbm, out_sem.at[0]),
+           pltpu.make_async_copy(before, change_hbm, out_sem.at[1])]
+    for copy in out:
+        copy.start()
     for copy in sent:
         copy.wait_send()
     for copy in stat:
         copy.wait_recv()
-    total = jnp.sum(gather[...], axis=0)
+    total_ref[...] = jnp.sum(gather[...], axis=0)
+    for copy in stat:
+        copy.wait_send()
+    for copy in out:
+        copy.wait()
+
+
+def lift_kernel(cells, total_ref, after, before, lifted_ref, diag_ref):
+    Z, X, Y = after.shape[1:]
+    wide = lax.broadcasted_iota(jnp.int32, (1, Y), 1)
+    total = total_ref[...]
     pick = lambda k: jnp.sum(jnp.where(wide == k, total, 0.0), axis=1, keepdims=True)
     t = [pick(k) for k in range(10)]
     change = (t[0] + t[1]) / cells
@@ -277,8 +301,6 @@
             even = base + 0.5 * (p * p)
             lifted_ref[i, z] = scaled[WEIGHTS[i]] * (even + p)
             lifted_ref[i + 1, z] = scaled[WEIGHTS[i]] * (even - p)
-    for copy in stat:
-        copy.wait_send()
 
 
 def solution(mesh):
@@ -291,11 +313,14 @@
         nzs = 1 if sizes["gz"] == 2 else 2
         count = 10 + 4 * nzs
         f32 = lambda *shape: pltpu.VMEM(shape, jnp.float32)
-        return pl.pallas_call(
-            functools.partial(kernel, sizes, float(Z * X * Y * n)),
-            out_shape=(jax.ShapeDtypeStruct(populations.shape, jnp.float32), jax.ShapeDtypeStruct((5,), jnp.float32)),
+        shape = lambda *dims: jax.ShapeDtypeStruct(dims, jnp.float32)
+        vmem, smem = pl.BlockSpec(memory_space=pltpu.VMEM), pl.BlockSpec(memory_space=pltpu.SMEM)
+        any_space = pl.BlockSpec(memory_space=pl.ANY)
+        total, after, change = pl.pallas_call(
+            functools.partial(kernel, sizes),
+            out_shape=(shape(1, Y), shape(4, Z, X, Y), shape(4, Z, X, Y)),
             in_specs=[pl.BlockSpec(memory_space=pl.ANY)] * 3,
-            out_specs=(pl.BlockSpec(memory_space=pltpu.VMEM), pl.BlockSpec(memory_space=pltpu.SMEM)),
+            out_specs=(vmem, any_space, any_space),
             scratch_shapes=[
                 f32(19, Z, X, Y), f32(Z, X, Y), pltpu.VMEM((Z, X, Y), jnp.int32),
                 f32(S, 19, Z, X, Y),
@@ -303,12 +328,18 @@
                 f32(S, 2, 5, Z, Y), f32(S, 2, X, Y), f32(S, 2, 5, X, Y),
                 f32(S, 2, 2, Z, Y), f32(S, 2, nzs, X, Y), f32(S, 2, nzs, X, Y),
                 f32(S, 2, 5, Z, Y), f32(4, Z, X, Y), f32(4, Z, X, Y), f32(n, 1, Y),
-                pltpu.SemaphoreType.DMA((Z + 2,)),
+                pltpu.SemaphoreType.DMA((Z + 2,)), pltpu.SemaphoreType.DMA((2,)),
                 pltpu.SemaphoreType.DMA((S, count)), pltpu.SemaphoreType.DMA((S, count)),
                 pltpu.SemaphoreType.DMA((n,)), pltpu.SemaphoreType.DMA((n,)),
             ],
             compiler_params=pltpu.CompilerParams(collective_id=0, has_side_effects=True),
         )(populations, omega, obstacle)
+        return pl.pallas_call(
+            functools.partial(lift_kernel, float(Z * X * Y * n)),
+            out_shape=(shape(*populations.shape), shape(5)),
+            in_specs=[vmem] * 3,
+            out_specs=(vmem, smem),
+        )(total, after, change)
 
     spec = P("gz", "gx", "gy")
     return jax.shard_map(

time: 36.2 us -> 35 us (0.967)
  local copies, waits for them, and re-layouts: 2.47 us -> 0 us
  Pallas kernels: 32.9 us -> 34.1 us
    unnamed x4 -> x0, local copies, waits for them, and re-layouts: 2.47 us -> none
    pallas_call x1 -> x2, Pallas kernels: 32.9 us -> 34.1 us  [the longest x1 32.1 us: per_device(): pl.pallas_call(functools.partial(kernel, sizes), out_shape=(shape(1, Y),...]
where the time goes in v2:
time: 35 us; the launch traced here: 34.8 us
  Pallas kernels  34.1 us (97%)
  between operations  0.64 us (2%)
    pallas_call x1, Pallas kernels, per_device(): pl.pallas_call(functools.partial(kernel, sizes), out_shape=(shape(1, Y),...  32.1 us
    pallas_call x1, Pallas kernels, per_device(): pl.pallas_call(functools.partial(lift_kernel, float(Z * X * Y * n)), out_...  2.04 us

profile of v2, /device:TPU:0, one launch (start us, length us, event | category | flops | bytes accessed | tf_op | source)
XLA Modules:
  0.0 34.8 jit_solution(6745151288320311083)
XLA Ops:
  0.6 32.1 %shard_map.50 = (f32[1,128]{1,0:T(1,128)}, f32[4,8,8,128]{3,2,1,0:T(8,128)}, f32[4,8,8,128]{3,2,1,0:T(8,128)}) custom-call(f32[19,8,8,128]{3,2,1,0:T(8,128)} %pop_hbm.1, f32[8,8,128]{2,1,0:T(8,128)} %omega_hbm.1, s32[8,8,128]{2,1,0:T(8,128)} %obstacle_hbm.1), custom_call_target="tpu_custom_call" | custom-call | tf_op jit(solution)/shard_map/pallas_call | solution.py:319
  32.7 2.0 %shard_map.51 = (f32[19,8,8,128]{3,2,1,0:T(8,128)}, f32[5]{0:T(128)}) custom-call(f32[1,128]{1,0:T(1,128)} %get-tuple-element.5.total_ref, f32[4,8,8,128]{3,2,1,0:T(8,128)} %get-tuple-element.6.after, f32[4,8,8,128]{3,2,1,0:T(8,128)} %get-tuple-element.7.before), custom_call_target="tpu_custom_call" | custom-call | tf_op jit(solution)/shard_map/pallas_call | solution.py:337

commit v3 on v2

--- a/solution.py
+++ b/solution.py
@@ -87,7 +87,7 @@
 
 
 def kernel(sizes, pop_hbm, omega_hbm, obstacle_hbm, total_ref, after_hbm, change_hbm,
-           f_in, om, ob, post, xs, ys, es, hx, hy, hz, hxy, hyz, hxz, cs, before, after, gather,
+           f_in, om, ob, post, xs, xc, ys, es, hx, hy, hz, hxy, hyz, hxz, cs, before, after, gather,
            load_sem, out_sem, send_sem, recv_sem, gsend_sem, grecv_sem):
     Z, X, Y = om.shape
     nx, ny, nz = (sizes[a] for a in AXES)
@@ -129,8 +129,7 @@
             out.append(((c, 0, 0), xs.at[s, d], hx.at[s, d]))
             out.append(((0, c, 0), ys.at[s, d], hy.at[s, d]))
             for b in (1, -1):
-                k = rank_in(0, INDEX[(c, b, 0)])
-                out.append(((c, b, 0), xs.at[s, d, k], hxy.at[s, d, side(b)]))
+                out.append(((c, b, 0), xc.at[s, d, side(b)], hxy.at[s, d, side(b)]))
             for b in zsides:
                 out.append(((0, c, b), ys.at[s, d], hyz.at[s, d, zside(b)]))
                 out.append(((c, 0, b), es.at[s, d], hxz.at[s, d, zside(b)]))
@@ -150,11 +149,15 @@
             edge = X - 1 if d == 0 else 0
             for k, i in enumerate(CROSS[0][d]):
                 xs[s, d, k] = post[s, SLOT[i], :, edge, :]
-            up = rank_in(0, INDEX[(1 - 2 * d, 0, 1)])
-            down = rank_in(0, INDEX[(1 - 2 * d, 0, -1)])
+            for b in (1, -1):
+                far_end = Y - 1 if b == 1 else 0
+                line = post[s, SLOT[INDEX[(1 - 2 * d, b, 0)]], :, edge, :][:, far_end:far_end + 1]
+                spots = jnp.where(zlane == zrow, jnp.broadcast_to(line, (Z, Y)), 0.0)
+                xc[s, d, side(b)] = jnp.sum(spots, axis=0, keepdims=True)
             first = post[s, SLOT[INDEX[(1 - 2 * d, 0, 1)]], Z - 1, edge:edge + 1, :]
             second = post[s, SLOT[INDEX[(1 - 2 * d, 0, -1)]], 0, edge:edge + 1, :]
-            es[s, d] = jnp.where(row == 0, jnp.broadcast_to(first, (X, Y)), jnp.broadcast_to(second, (X, Y)))
+            es[s, d, 0] = first
+            es[s, d, 1] = second
 
     def pack_y(s):
         for d in (0, 1):
@@ -174,12 +177,13 @@
                 col = hx[s, d, k]
                 if cy:
                     edge = 0 if cy == 1 else Y - 1
-                    corner = pltpu.roll(hxy[s, d, side(cy)], cy % Y, 1)
+                    spots = jnp.where(zlane == zrow, jnp.broadcast_to(hxy[s, d, side(cy)], (Z, Y)), 0.0)
+                    corner = jnp.broadcast_to(jnp.sum(spots, axis=1, keepdims=True), (Z, Y))
                     col = jnp.where(zlane == edge, corner, pltpu.roll(col, cy % Y, 1))
                 if cz:
                     edge = 0 if cz == 1 else Z - 1
                     r = 0 if cz == 1 else 1
-                    corner = jnp.broadcast_to(hxz[s, d, zside(cz), r:r + 1, :], (Z, Y))
+                    corner = jnp.broadcast_to(hxz[s, d, zside(cz), r], (Z, Y))
                     col = jnp.where(zrow == edge, corner, pltpu.roll(col, cz % Z, 0))
                 cs[s, d, k] = col
 
@@ -324,9 +328,9 @@
             scratch_shapes=[
                 f32(19, Z, X, Y), f32(Z, X, Y), pltpu.VMEM((Z, X, Y), jnp.int32),
                 f32(S, 19, Z, X, Y),
-                f32(S, 2, 5, Z, Y), f32(S, 2, X, Y), f32(S, 2, X, Y),
+                f32(S, 2, 5, Z, Y), f32(S, 2, 2, 1, Y), f32(S, 2, X, Y), f32(S, 2, 2, 1, Y),
                 f32(S, 2, 5, Z, Y), f32(S, 2, X, Y), f32(S, 2, 5, X, Y),
-                f32(S, 2, 2, Z, Y), f32(S, 2, nzs, X, Y), f32(S, 2, nzs, X, Y),
+                f32(S, 2, 2, 1, Y), f32(S, 2, nzs, X, Y), f32(S, 2, nzs, 2, 1, Y),
                 f32(S, 2, 5, Z, Y), f32(4, Z, X, Y), f32(4, Z, X, Y), f32(n, 1, Y),
                 pltpu.SemaphoreType.DMA((Z + 2,)), pltpu.SemaphoreType.DMA((2,)),
                 pltpu.SemaphoreType.DMA((S, count)), pltpu.SemaphoreType.DMA((S, count)),

time: 35 us -> 34.5 us (0.986)
  Pallas kernels: 34.1 us -> 33.7 us
    pallas_call x1, Pallas kernels: 32.1 us -> 31.6 us  [per_device(): pl.pallas_call(functools.partial(kernel, sizes), out_shape=(shape(1, Y),...]
where the time goes in v3:
time: 34.5 us; the launch traced here: 34.3 us
  Pallas kernels  33.7 us (98%)
  between operations  0.64 us (2%)
    pallas_call x1, Pallas kernels, per_device(): pl.pallas_call(functools.partial(kernel, sizes), out_shape=(shape(1, Y),...  31.6 us
    pallas_call x1, Pallas kernels, per_device(): pl.pallas_call(functools.partial(lift_kernel, float(Z * X * Y * n)), out_...  2.04 us

profile of v3, /device:TPU:0, one launch (start us, length us, event | category | flops | bytes accessed | tf_op | source)
XLA Modules:
  0.0 34.3 jit_solution(2951235291512119094)
XLA Ops:
  0.6 31.6 %shard_map.50 = (f32[1,128]{1,0:T(1,128)}, f32[4,8,8,128]{3,2,1,0:T(8,128)}, f32[4,8,8,128]{3,2,1,0:T(8,128)}) custom-call(f32[19,8,8,128]{3,2,1,0:T(8,128)} %pop_hbm.1, f32[8,8,128]{2,1,0:T(8,128)} %omega_hbm.1, s32[8,8,128]{2,1,0:T(8,128)} %obstacle_hbm.1), custom_call_target="tpu_custom_call" | custom-call | tf_op jit(solution)/shard_map/pallas_call | solution.py:323
  32.2 2.0 %shard_map.51 = (f32[19,8,8,128]{3,2,1,0:T(8,128)}, f32[5]{0:T(128)}) custom-call(f32[1,128]{1,0:T(1,128)} %get-tuple-element.5.total_ref, f32[4,8,8,128]{3,2,1,0:T(8,128)} %get-tuple-element.6.after, f32[4,8,8,128]{3,2,1,0:T(8,128)} %get-tuple-element.7.before), custom_call_target="tpu_custom_call" | custom-call | tf_op jit(solution)/shard_map/pallas_call | solution.py:341

commit v4 on v3

--- a/solution.py
+++ b/solution.py
@@ -225,10 +225,12 @@
             for i in range(19):
                 post[s, SLOT[i], z] = new[i]
         along_x, along_z, along_y = messages(s)
-        pack_x(s)
         if s == 0:
             pl.semaphore_wait(barrier, len(greet))
-        for copy in along_x + along_z:
+        for copy in along_z:
+            copy.start()
+        pack_x(s)
+        for copy in along_x:
             copy.start()
         pack_y(s)
         for copy in along_y:
@@ -261,7 +263,8 @@
     slot = (me[0] * ny + me[1]) * nz + me[2]
     gather[slot] = mine
     stat = []
-    for k, offset in enumerate(everyone):
+    hops = lambda o: sum(min(c, m - c) for c, m in zip(o, (nx, ny, nz)))
+    for k, offset in enumerate(sorted(everyone, key=lambda o: -hops(o))):
         stat.append(pltpu.make_async_remote_copy(
             src_ref=gather.at[slot], dst_ref=gather.at[slot], send_sem=gsend_sem.at[k], recv_sem=grecv_sem.at[k],
             device_id=device(offset), device_id_type=pl.DeviceIdType.MESH))

time: 34.5 us -> 34.5 us (level)
  no operation moved by 1% of the time
where the time goes in v4:
time: 34.5 us; the launch traced here: 34.3 us
  Pallas kernels  33.7 us (98%)
  between operations  0.64 us (2%)
    pallas_call x1, Pallas kernels, per_device(): pl.pallas_call(functools.partial(kernel, sizes), out_shape=(shape(1, Y),...  31.6 us
    pallas_call x1, Pallas kernels, per_device(): pl.pallas_call(functools.partial(lift_kernel, float(Z * X * Y * n)), out_...  2.04 us

profile of v4, /device:TPU:0, one launch (start us, length us, event | category | flops | bytes accessed | tf_op | source)
XLA Modules:
  0.0 34.3 jit_solution(5114918875600101185)
XLA Ops:
  0.6 31.6 %shard_map.50 = (f32[1,128]{1,0:T(1,128)}, f32[4,8,8,128]{3,2,1,0:T(8,128)}, f32[4,8,8,128]{3,2,1,0:T(8,128)}) custom-call(f32[19,8,8,128]{3,2,1,0:T(8,128)} %pop_hbm.1, f32[8,8,128]{2,1,0:T(8,128)} %omega_hbm.1, s32[8,8,128]{2,1,0:T(8,128)} %obstacle_hbm.1), custom_call_target="tpu_custom_call" | custom-call | tf_op jit(solution)/shard_map/pallas_call | solution.py:326
  32.3 2.0 %shard_map.51 = (f32[19,8,8,128]{3,2,1,0:T(8,128)}, f32[5]{0:T(128)}) custom-call(f32[1,128]{1,0:T(1,128)} %get-tuple-element.5.total_ref, f32[4,8,8,128]{3,2,1,0:T(8,128)} %get-tuple-element.6.after, f32[4,8,8,128]{3,2,1,0:T(8,128)} %get-tuple-element.7.before), custom_call_target="tpu_custom_call" | custom-call | tf_op jit(solution)/shard_map/pallas_call | solution.py:344
